TPU v7x, 32 devices: a whole 2x2x4 slice. The times are simulated.
32 devices in a mesh: prow: 8 (over z, x), pcol: 4 (over y, core).
Axes of the slice: x: 2, y: 2, z: 4, core: 2. Of those that a mesh axis runs over, the one named last changes fastest.
Arguments:
- a_matrix: bfloat16 [32768, 512], P('prow', 'pcol'), may hold values from -6 to 6
- l_panel: bfloat16 [32768, 256], P('prow', 'pcol'), may hold values from -0.375 to 0.375
- l_inverse: bfloat16 [256, 256], replicated, may hold values from -1 to 1
- pivots: int32 [256], replicated, may hold values from 0 to 32767, as said below
Outputs:
- updated: bfloat16 [32768, 512], P('prow', 'pcol')
Inputs may be any that keep to these rules, and one draw needn't show every extreme that they name: pivots[j] >= j for every j.
All inputs are finite; a program needn't handle non-finite values.
Results may differ from a plain program's by a relative error of at most 0.0039.
Values may be sent and summed in bfloat16 or wider, within the bound.
A program may use at most 64 MiB of HBM per device.

v0:
```python
import jax
import jax.numpy as jnp
from jax import lax
from jax.sharding import PartitionSpec as P


def swap_plan(pivots, panel_width):
    slot_ids = jnp.arange(panel_width, dtype=jnp.int32)
    earlier = slot_ids[None, :] < slot_ids[:, None]
    hits = (pivots[None, :] == slot_ids[:, None]) & earlier
    pointer = jnp.max(jnp.where(hits, slot_ids[None, :], -1), axis=1)
    chain = jnp.where(pointer >= 0, pointer, slot_ids)
    for _ in range(panel_width.bit_length()):
        chain = jnp.take(chain, chain)
    same = pivots[None, :] == pivots[:, None]
    previous = jnp.max(jnp.where(same & earlier, slot_ids[None, :], -1), axis=1)
    top_source = jnp.where(previous >= 0, jnp.take(chain, jnp.maximum(previous, 0)), pivots)
    later = slot_ids[None, :] > slot_ids[:, None]
    is_last = jnp.logical_not(jnp.any(same & later, axis=1))
    return (top_source, chain, is_last)


def body(a_matrix, l_panel, l_inverse, pivots):
    local_count, col_count = a_matrix.shape
    panel_width = l_inverse.shape[0]
    prow_count = lax.axis_size("prow")
    prow_index = lax.axis_index("prow")
    top_source, moved_source, is_last = swap_plan(pivots, panel_width)
    local_rows = jnp.arange(local_count, dtype=jnp.int32)
    global_rows = (
        local_rows // panel_width * prow_count + prow_index
    ) * panel_width + local_rows % panel_width

    def owner_of(wanted):
        return wanted // panel_width % prow_count

    def local_of(wanted):
        return wanted // (panel_width * prow_count) * panel_width + wanted % panel_width

    def owned_part(wanted, usable):
        taken = jnp.take(a_matrix, local_of(wanted), axis=0).astype(jnp.float32)
        return jnp.where(
            ((owner_of(wanted) == prow_index) & usable)[:, None], taken, jnp.zeros((), jnp.float32)
        )

    usable_moves = is_last & (pivots >= panel_width)
    top_part = owned_part(top_source, jnp.ones((panel_width,), jnp.bool_))
    moved_part = owned_part(moved_source, usable_moves)
    moved_rows = lax.psum(moved_part, "prow")
    landing = jnp.where(
        usable_moves & (owner_of(pivots) == prow_index), local_of(pivots), local_count
    )
    swapped = a_matrix.at[landing].set(moved_rows.astype(jnp.bfloat16), mode="drop")
    top_rows = lax.psum(top_part, "prow")
    u_block = jnp.dot(
        l_inverse, top_rows.astype(jnp.bfloat16), preferred_element_type=jnp.float32
    ).astype(jnp.bfloat16)
    panel_full = lax.all_gather(l_panel, "pcol", axis=1, tiled=True)
    update = jnp.dot(panel_full, u_block, preferred_element_type=jnp.float32)
    updated = (swapped.astype(jnp.float32) - update).astype(jnp.bfloat16)
    u_padded = jnp.concatenate(
        [u_block, jnp.zeros((local_count - panel_width, col_count), jnp.bfloat16)], axis=0
    )
    return jnp.where((global_rows < panel_width)[:, None], u_padded, updated)


def solution(mesh):
    in_specs = (P("prow", "pcol"), P("prow", "pcol"), P(), P())
    out_specs = P("prow", "pcol")
    return jax.shard_map(body, mesh=mesh, in_specs=in_specs, out_specs=out_specs, check_vma=False)
```

profile of v0, /device:TPU:0, one launch (start us, length us, event | category | flops | bytes accessed | tf_op | source)
XLA Modules:
  0.0 115.9 jit_solution(2225911435671411788)
XLA Ops:
  7.4 0.0 copy-start
  7.4 0.0 copy-start.1
  7.4 0.0 all-reduce.4.cloned.1.call-start
  7.4 1.3 %copy.16 = bf16[4096,128]{1,0:T(8,128)(2,1)S(1)} copy(bf16[4096,128]{1,0:T(8,128)(2,1)} %param.8) | data formatting | bytes 2097152
  8.6 0.0 copy-done.1
  8.6 0.2 select_reduce_fusion
  8.9 0.2 fusion.4
  9.1 1.9 %gather_fusion = s32[256]{0:T(256)S(1)} fusion(s32[256]{0:T(256)S(1)} %get-tuple-element.34, s32[1024]{0:T(1024)S(1)} %pad_clamp_fusion.11), kind=kCustom, calls=%fused_computation.clone | custom fusion | bytes 3072 | tf_op jit(solution)/shard_map/jit(_take)/gather | solution.py:14
  11.0 1.9 %gather_fusion.1 = s32[256]{0:T(256)S(1)} fusion(s32[256]{0:T(256)S(1)} %get-tuple-element.32, s32[1024]{0:T(1024)S(1)} %pad_clamp_fusion.10), kind=kCustom, calls=%fused_computation.2.clone | custom fusion | bytes 3072 | tf_op jit(solution)/shard_map/jit(_take)/gather | solution.py:14
  13.0 1.9 %gather_fusion.2 = s32[256]{0:T(256)S(1)} fusion(s32[256]{0:T(256)S(1)} %get-tuple-element.30, s32[1024]{0:T(1024)S(1)} %pad_clamp_fusion.9), kind=kCustom, calls=%fused_computation.3.clone | custom fusion | bytes 3072 | tf_op jit(solution)/shard_map/jit(_take)/gather | solution.py:14
  15.0 1.9 %gather_fusion.3 = s32[256]{0:T(256)S(1)} fusion(s32[256]{0:T(256)S(1)} %get-tuple-element.28, s32[1024]{0:T(1024)S(1)} %pad_clamp_fusion.8), kind=kCustom, calls=%fused_computation.4.clone | custom fusion | bytes 3072 | tf_op jit(solution)/shard_map/jit(_take)/gather | solution.py:14
  17.0 1.9 %gather_fusion.4 = s32[256]{0:T(256)S(1)} fusion(s32[256]{0:T(256)S(1)} %get-tuple-element.26, s32[1024]{0:T(1024)S(1)} %pad_clamp_fusion.7), kind=kCustom, calls=%fused_computation.5.clone | custom fusion | bytes 3072 | tf_op jit(solution)/shard_map/jit(_take)/gather | solution.py:14
  19.0 1.9 %gather_fusion.5 = s32[256]{0:T(256)S(1)} fusion(s32[256]{0:T(256)S(1)} %get-tuple-element.24, s32[1024]{0:T(1024)S(1)} %pad_clamp_fusion.6), kind=kCustom, calls=%fused_computation.6.clone | custom fusion | bytes 3072 | tf_op jit(solution)/shard_map/jit(_take)/gather | solution.py:14
  21.0 1.9 %gather_fusion.6 = s32[256]{0:T(256)S(1)} fusion(s32[256]{0:T(256)S(1)} %get-tuple-element.22, s32[1024]{0:T(1024)S(1)} %pad_clamp_fusion.5), kind=kCustom, calls=%fused_computation.7.clone | custom fusion | bytes 3072 | tf_op jit(solution)/shard_map/jit(_take)/gather | solution.py:14
  23.0 1.9 %gather_fusion.7 = s32[256]{0:T(256)S(1)} fusion(s32[256]{0:T(256)S(1)} %get-tuple-element.20, s32[1024]{0:T(1024)S(1)} %pad_clamp_fusion.4), kind=kCustom, calls=%fused_computation.8.clone | custom fusion | bytes 3072 | tf_op jit(solution)/shard_map/jit(_take)/gather | solution.py:14
  25.0 1.9 %gather_fusion.8 = s32[256]{0:T(256)S(1)} fusion(s32[256]{0:T(256)S(1)} %get-tuple-element.18, s32[1024]{0:T(1024)S(1)} %pad_clamp_fusion.3), kind=kCustom, calls=%fused_computation.9.clone | custom fusion | bytes 3072 | tf_op jit(solution)/shard_map/jit(_take)/gather | solution.py:14
  27.0 0.9 gather_fusion.11
  27.8 0.8 convert_select_fusion
  28.6 0.0 all-reduce.4.cloned.1.call-update
  28.6 0.0 all-gather.2.cloned.1.call-start
  28.7 0.5 all-gather.2.cloned.1.call-update
  29.2 1.9 %gather_fusion.9 = s32[256]{0:T(256)S(1)} fusion(s32[256]{0:T(256)S(1)} %get-tuple-element.10, s32[1024]{0:T(1024)S(1)} %pad_clamp_fusion.2), kind=kCustom, calls=%fused_computation.10.clone | custom fusion | bytes 3072 | tf_op jit(solution)/shard_map/jit(_take)/gather | solution.py:17
  31.3 0.9 gather_fusion.10
  32.1 0.1 convert_select_fusion.1
  32.3 40.3 %all-reduce.5 = bf16[256,128]{1,0:T(8,128)(2,1)S(1)} all-reduce(f32[256,128]{1,0:T(8,128)S(1)} %convert_select_fusion.1), channel_id=1, replica_groups=mesh['prow'=8,'pcol'=4] {'prow'}, use_global_device_ids=true, to_apply=%region_2.5 | all-reduce | flops 32768 | bytes 196608 | tf_op jit(solution)/shard_map/psum | solution.py:54
  72.6 0.0 copy-done
  72.6 0.2 convolution_convert_fusion
  72.8 29.3 %all-reduce.4.cloned.1.call-done = f32[256,128]{1,0:T(8,128)} async-done(((f32[256,128]{1,0:T(8,128)}), f32[256,128]{1,0:T(8,128)}) %all-reduce.4.cloned.1.call-update) | async-done | bytes 131088 | tf_op jit(solution)/shard_map/psum | solution.py:49
  102.1 2.2 %scatter_custom_fusion = bf16[4096,128]{1,0:T(8,128)(2,1)S(1)} fusion(bf16[4096,128]{1,0:T(8,128)(2,1)S(1)} %copy.16, s32[256]{0:T(256)S(1)} %compare_select_fusion.11, f32[256,128]{1,0:T(8,128)} %all-reduce.4.cloned.1.call-done), kind=kCustom, calls=%fused_computation.29 | custom fusion | flops 32768 | bytes 1179648 | tf_op jit(solution)/shard_map/scatter | solution.py:53
  104.3 0.5 copy.9
  104.8 0.0 all-gather.2.cloned.1.call-done
  104.9 2.2 %fusion.2 = bf16[4096,128]{0,1:T(8,128)(2,1)S(1)} fusion(bf16[128,256]{1,0:T(8,128)(2,1)S(1)} %convolution_convert_fusion, bf16[4096,256]{0,1:T(8,128)(2,1)} %all-gather.2.cloned.1.call-done, bf16[4096,128]{0,1:T(8,128)(2,1)S(1)} %copy.9, bf16[256,128]{0,1:T(8,128)(2,1)S(1)} %bitcast.13, pred[4096]{0:T(1024)(128)(4,1)S(1)} %fusion.18), kind=kOutput, calls=%fused_computation.16 | convolution fusion | flops 270532608 | bytes 4329472 | tf_op jit(solution)/shard_map/dot_general | solution.py:59
  107.1 1.3 %copy.10 = bf16[4096,128]{1,0:T(8,128)(2,1)} copy(bf16[4096,128]{0,1:T(8,128)(2,1)S(1)} %fusion.2) | data formatting | bytes 2097152 | tf_op jit(solution)/shard_map/jit(_where)/select_n | solution.py:64
  (27 shorter events, 0.3 us)
Async XLA Ops:
  7.4 65.2 %copy-start = (bf16[256,256]{1,0:T(8,128)(2,1)S(1)}, bf16[256,256]{1,0:T(8,128)(2,1)}, u32[]{:S(2)}) copy-start(bf16[256,256]{1,0:T(8,128)(2,1)} %param.10) | copy-start | bytes 393220
  7.4 1.3 %copy-start.1 = (s32[256]{0:T(256)S(1)}, s32[256]{0:T(256)}, u32[]{:S(2)}) copy-start(s32[256]{0:T(256)} %param.11) | copy-start | bytes 3076
  7.4 94.8 %all-reduce.4.cloned.1.call-start = ((), (), s32[]{:S(2)}) async-start(), calls=%async_computation | async-start | bytes 262144 | tf_op jit(solution)/shard_map/psum | solution.py:49
  28.6 76.2 %all-gather.2.cloned.1.call-start = ((), (), s32[]{:S(2)}) async-start(), calls=%async_computation.1 | async-start | bytes 2621440 | tf_op jit(solution)/shard_map/all_gather | solution.py:58
Sparse Core Ops, SparseCore 0:
  28.8 73.3 all-reduce.3
Sparse Core Ops, SparseCore 1:
  30.7 25.1 all-gather.1
where the time goes:
time: 116 us
  blocking collectives  40.3 us (35%)
  waiting for transfers between devices  29.9 us (26%)
  local copies, waits for them, and re-layouts  24.3 us (21%)
  between operations  15.2 us (13%)
  other arithmetic  3.71 us (3%)
  matrix products  2.41 us (2%)
    psum x1, blocking collectives, body(): top_rows = lax.psum(top_part, 'prow')  40.3 us
    psum x1, waiting for transfers between devices, body(): moved_rows = lax.psum(moved_part, 'prow')  29.3 us
    gather x9, local copies, waits for them, and re-layouts, swap_plan(): chain = jnp.take(chain, chain)  17.6 us
  transfers between devices with their start and end apart: 2, of which 1 were waited for; matrix products, arithmetic and copies ran while one was open for 5% of the time, Pallas kernels for 0%

commit v1 on v0

v1 whole, which is shorter than its diff:
```python
import functools

import jax
import jax.numpy as jnp
from jax import lax
from jax.experimental import pallas as pl
from jax.experimental.pallas import tpu as pltpu
from jax.sharding import PartitionSpec as P

MESH = pl.DeviceIdType.MESH
F32 = jnp.float32
BF16 = jnp.bfloat16
CORES = 2


def one_hot(mask):
    return jnp.where(mask, 1.0, 0.0).astype(BF16)


def swap_plan(pv_row):
    nb = pv_row.shape[1]
    slot = lax.broadcasted_iota(jnp.int32, (nb, nb), 0).astype(F32)
    other = lax.broadcasted_iota(jnp.int32, (nb, nb), 1).astype(F32)
    slot_col = lax.broadcasted_iota(jnp.int32, (nb, 1), 0).astype(F32)
    earlier = other < slot
    pv_col = jnp.max(jnp.where(slot == other, pv_row, -1.0), axis=1, keepdims=True)
    pointer = jnp.max(jnp.where((pv_row == slot) & earlier, other, -1.0), axis=1, keepdims=True)
    chain = one_hot(other == jnp.where(pointer >= 0, pointer, slot_col))
    for _ in range((nb - 1).bit_length()):
        chain = jnp.dot(chain, chain, preferred_element_type=F32).astype(BF16)
    same = pv_row == pv_col
    previous = jnp.max(jnp.where(same & earlier, other, -1.0), axis=1, keepdims=True)
    via = jnp.dot(one_hot(other == previous), chain, preferred_element_type=F32)
    via_chain = jnp.max(jnp.where(via > 0.5, other, -1.0), axis=1, keepdims=True)
    top_source = jnp.where(previous >= 0, via_chain, pv_col)
    repeated = jnp.max(jnp.where(same & (slot > other), 1.0, 0.0), axis=0, keepdims=True)
    landing = jnp.where((repeated < 0.5) & (pv_row >= nb), pv_row, -1.0)
    return top_source, chain, landing


def kernel(
    n_prow, n_pcol, chunks,
    a_hbm, l_hbm, inv_hbm, pv_ref, out_hbm,
    a_v, l_full, inv_v, out_v, part, got, mine, tops, origs,
    load_sem, out_sem, own_sem,
    p1_send, p1_recv, p2_send, p2_recv, o1_send, o1_recv, o2_send, o2_recv,
    y_send, y_recv, m_send, m_recv, f_send, f_recv,
):
    rows, width = a_v.shape
    nb = inv_v.shape[0]
    n_red, piece, _ = part.shape
    step = rows // chunks
    n_y = n_pcol // CORES
    me = lax.axis_index("prow")
    col = lax.axis_index("pcol")
    y, core = col // CORES, col % CORES
    mate = y * CORES + (1 - core)

    def y_peer(d):
        return lax.rem(y + d, n_y) * CORES + core

    def y_from(d):
        return lax.rem(y + n_y - d, n_y) * CORES + core

    def to(d):
        return lax.rem(me + d, n_prow)

    def frm(d):
        return lax.rem(me + n_prow - d, n_prow)

    def if_red(index, fn):
        if n_red == n_prow:
            fn()
        else:
            pl.when(index < n_red)(fn)

    l_load = pltpu.make_async_copy(l_hbm, l_full.at[col], load_sem.at[0])
    a_load = pltpu.make_async_copy(a_hbm, a_v, load_sem.at[1])
    inv_load = pltpu.make_async_copy(inv_hbm, inv_v, load_sem.at[2])
    l_load.start()
    a_load.start()
    inv_load.start()

    barrier = pltpu.get_barrier_semaphore()
    for d in range(1, n_prow):
        pl.semaphore_signal(barrier, inc=1, device_id=(to(d), col), device_id_type=MESH)
    for d in range(1, n_y):
        pl.semaphore_signal(barrier, inc=1, device_id=(me, y_peer(d)), device_id_type=MESH)
    pl.semaphore_signal(barrier, inc=1, device_id=(me, mate), device_id_type=MESH)

    top_source, chain, landing = swap_plan(pv_ref[...].astype(F32))

    l_load.wait()
    pl.semaphore_wait(barrier, n_prow - 1 + n_y - 1 + 1)

    def cols(k):
        return pl.ds(k * step, step)

    y_copies = {}
    for k in range(chunks):
        for d in range(1, n_y):
            y_copies[d, k] = pltpu.make_async_remote_copy(
                l_full.at[col, :, cols(k)], l_full.at[col, :, cols(k)],
                y_send.at[d, k], y_recv.at[d, k], device_id=(me, y_peer(d)), device_id_type=MESH)
            y_copies[d, k].start()
    m_copy = pltpu.make_async_remote_copy(
        l_full.at[col], l_full.at[col], m_send, m_recv, device_id=(me, mate), device_id_type=MESH)

    a_load.wait()
    o1_copies = [
        pltpu.make_async_remote_copy(
            a_v.at[pl.ds(d * piece, piece)], origs.at[d], o1_send.at[d], o1_recv,
            device_id=(d, col), device_id_type=MESH)
        for d in range(1, n_red)
    ]
    own_copy = pltpu.make_async_copy(a_v.at[pl.ds(0, piece)], origs.at[0], own_sem)

    @pl.when(me == 0)
    def _():
        for copy in o1_copies:
            copy.start()
        own_copy.start()

    m_copy.start()

    def global_rows(shape, axis, start):
        local = lax.broadcasted_iota(jnp.int32, shape, axis) + start
        return ((local // nb * n_prow + me) * nb + local % nb).astype(F32)

    total = jnp.zeros((nb, width), F32)
    for k in range(chunks):
        pick = one_hot(top_source == global_rows((1, step), 1, k * step))
        total = total + jnp.dot(pick, a_v[pl.ds(k * step, step), :], preferred_element_type=F32)
    part[...] = total.astype(BF16).reshape(n_red, piece, width)

    p1_copies = {}
    for d in range(1, n_prow):
        t = to(d)
        p1_copies[d] = pltpu.make_async_remote_copy(
            part.at[lax.rem(t, n_red)], got.at[d], p1_send.at[d], p1_recv.at[d],
            device_id=(t, col), device_id_type=MESH)
        if_red(t, p1_copies[d].start)

    slot = lax.rem(me, n_red)
    o2_copies, p2_copies = {}, {}
    for d in range(1, n_prow):
        o2_copies[d] = pltpu.make_async_remote_copy(
            origs.at[slot], origs.at[slot], o2_send.at[d], o2_recv.at[d],
            device_id=(to(d), col), device_id_type=MESH)
        p2_copies[d] = pltpu.make_async_remote_copy(
            mine, tops.at[slot], p2_send.at[d], p2_recv.at[d],
            device_id=(to(d), col), device_id_type=MESH)

    @pl.when(me == 0)
    def _():
        own_copy.wait()

    @pl.when((me > 0) & (me < n_red))
    def _():
        o1_copies[0].wait_recv()

    def send_orig():
        for d in range(1, n_prow):
            o2_copies[d].start()

    if_red(me, send_orig)

    def reduce_and_send():
        acc = part[slot].astype(F32)
        for d in range(1, n_prow):
            p1_copies[d].wait_recv()
            acc = acc + got[d].astype(F32)
        mine[...] = acc.astype(BF16)
        tops[slot] = acc.astype(BF16)
        for d in range(1, n_prow):
            p2_copies[d].start()

    if_red(me, reduce_and_send)

    for d in range(1, n_prow):
        if_red(frm(d), o2_copies[d].wait_recv)
    moved = jnp.dot(chain, origs[...].reshape(nb, width), preferred_element_type=F32).astype(BF16)
    moved = jnp.concatenate([moved, jnp.ones((nb, width), BF16)], axis=1)
    for k in range(chunks):
        here = one_hot(landing == global_rows((step, 1), 0, k * step))
        both = jnp.dot(here, moved, preferred_element_type=F32)
        rows_k = pl.ds(k * step, step)
        out_v[rows_k, :] = jnp.where(
            both[:, width:] > 0.5, both[:, :width], a_v[rows_k, :].astype(F32)).astype(BF16)

    for d in range(1, n_prow):
        if_red(frm(d), p2_copies[d].wait_recv)
    inv_load.wait()
    u_block = jnp.dot(
        inv_v[...], tops[...].reshape(nb, width), preferred_element_type=F32).astype(BF16)

    f_copies = {}

    def forward(k):
        for d in range(1, n_y):
            y_copies[d, k].wait_recv()
            src = y_from(d)
            f_copies[d, k] = pltpu.make_async_remote_copy(
                l_full.at[src, :, cols(k)], l_full.at[src, :, cols(k)],
                f_send.at[d, k], f_recv.at[d, k], device_id=(me, mate), device_id_type=MESH)
            f_copies[d, k].start()

    out_copies = []

    def finish(k):
        for d in range(1, n_y):
            f_copies[d, k].wait_recv()
        rows_k = pl.ds(k * step, step)
        panel = l_full[:, :, cols(k)].reshape(nb, step)
        update = lax.dot_general(
            panel, u_block, (((0,), (0,)), ((), ())), preferred_element_type=F32)
        out_v[rows_k, :] = (out_v[rows_k, :].astype(F32) - update).astype(BF16)
        top = min(step, nb - k * step)
        if top > 0:
            @pl.when(me == 0)
            def _():
                out_v[pl.ds(k * step, top), :] = u_block[k * step:k * step + top, :]
        copy = pltpu.make_async_copy(out_v.at[rows_k], out_hbm.at[rows_k], out_sem.at[k])
        copy.start()
        out_copies.append(copy)

    forward(0)
    m_copy.wait_recv()
    for k in range(1, chunks):
        forward(k)
        finish(k - 1)
    finish(chunks - 1)

    @pl.when(me == 0)
    def _():
        for copy in o1_copies:
            copy.wait_send()

    m_copy.wait_send()
    for d in range(1, n_prow):
        if_red(to(d), p1_copies[d].wait_send)

    def drain():
        for d in range(1, n_prow):
            o2_copies[d].wait_send()
            p2_copies[d].wait_send()

    if_red(me, drain)
    for key in y_copies:
        y_copies[key].wait_send()
        f_copies[key].wait_send()
    for copy in out_copies:
        copy.wait()


def body(n_prow, n_pcol, a_matrix, l_panel, l_inverse, pivots):
    rows, width = a_matrix.shape
    nb = l_inverse.shape[0]
    depth = l_panel.shape[1]
    piece = max(16, nb // n_prow)
    n_red = nb // piece
    n_y = n_pcol // CORES
    chunks = min(8, rows // 128)
    dma = pltpu.SemaphoreType.DMA
    return pl.pallas_call(
        functools.partial(kernel, n_prow, n_pcol, chunks),
        out_shape=jax.ShapeDtypeStruct((rows, width), BF16),
        in_specs=[pl.BlockSpec(memory_space=pl.ANY)] * 3 + [pl.BlockSpec(memory_space=pltpu.VMEM)],
        out_specs=pl.BlockSpec(memory_space=pl.ANY),
        scratch_shapes=[
            pltpu.VMEM((rows, width), BF16),
            pltpu.VMEM((n_pcol, depth, rows), BF16),
            pltpu.VMEM((nb, nb), BF16),
            pltpu.VMEM((rows, width), BF16),
            pltpu.VMEM((n_red, piece, width), BF16),
            pltpu.VMEM((n_prow, piece, width), BF16),
            pltpu.VMEM((piece, width), BF16),
            pltpu.VMEM((n_red, piece, width), BF16),
            pltpu.VMEM((n_red, piece, width), BF16),
            dma((3,)), dma((chunks,)), dma,
            dma((n_prow,)), dma((n_prow,)), dma((n_prow,)), dma((n_prow,)),
            dma((n_red,)), dma, dma((n_prow,)), dma((n_prow,)),
            dma((n_y, chunks)), dma((n_y, chunks)), dma, dma,
            dma((n_y, chunks)), dma((n_y, chunks)),
        ],
        compiler_params=pltpu.CompilerParams(
            collective_id=0, has_side_effects=True, vmem_limit_bytes=24 * 2 ** 20),
    )(a_matrix, l_panel.T, l_inverse, pivots.reshape(1, nb))


def solution(mesh):
    n_prow, n_pcol = mesh.shape["prow"], mesh.shape["pcol"]
    in_specs = (P("prow", "pcol"), P("prow", "pcol"), P(), P())
    return jax.shard_map(
        functools.partial(body, n_prow, n_pcol),
        mesh=mesh, in_specs=in_specs, out_specs=P("prow", "pcol"), check_vma=False)
```

time: 116 us -> 29.6 us (0.26)
  blocking collectives: 40.3 us -> 0 us
  waiting for transfers between devices: 29.9 us -> 0 us
  Pallas kernels: 0 us -> 24.6 us
  local copies, waits for them, and re-layouts: 24.3 us -> 4.82 us
  between operations: 15.2 us -> 0.01 us
  other arithmetic: 3.71 us -> 0 us
  matrix products: 2.41 us -> 0 us
    psum x1 -> x0, blocking collectives: 40.3 us -> none  [body(): top_rows = lax.psum(top_part, 'prow')]
    psum x1 -> x0, waiting for transfers between devices: 29.3 us -> none  [body(): moved_rows = lax.psum(moved_part, 'prow')]
    pallas_call x0 -> x1, Pallas kernels: none -> 24.6 us  [body(): pl.pallas_call(functools.partial(kernel, n_prow, n_pcol, chunks), out_sha...]
    gather x12 -> x0, local copies, waits for them, and re-layouts: 21.2 us -> none  [the longest x9 17.6 us: swap_plan(): chain = jnp.take(chain, chain)]
    unnamed x5 -> x9, local copies, waits for them, and re-layouts: 1.28 us -> 4.82 us
    dot_general x2 -> x0, matrix products: 2.41 us -> none  [the longest x1 2.22 us: body(): update = jnp.dot(panel_full, u_block, preferred_element_type=jnp.float32)]
    scatter x1 -> x0, other arithmetic: 2.15 us -> none  [body(): a_matrix.at[landing].set(moved_rows.astype(jnp.bfloat16), mode='drop')]
    select_n x1 -> x0, local copies, waits for them, and re-layouts: 1.31 us -> none  [body(): return jnp.where((global_rows < panel_width)[:, None], u_padded, updated)]
  transfers between devices with their start and end apart: 2 -> 0, of which waited for: 1 -> 0; matrix products, arithmetic and copies ran while one was open for 5% -> 0% of each run, Pallas kernels for 0% -> 0%
where the time goes in v1:
time: 29.6 us; the launch traced here: 29.4 us
  Pallas kernels  24.6 us (83%)
  local copies, waits for them, and re-layouts  4.82 us (16%)
    pallas_call x1, Pallas kernels, body(): pl.pallas_call(functools.partial(kernel, n_prow, n_pcol, chunks), out_sha...  24.6 us
    unnamed x9, local copies, waits for them, and re-layouts  4.82 us

profile of v1, /device:TPU:0, one launch (start us, length us, event | category | flops | bytes accessed | tf_op | source)
XLA Modules:
  0.0 29.4 jit_solution(1429724320754619652)
XLA Ops:
  0.0 0.0 copy-start.3
  0.0 0.7 %copy-done.3 = s32[256]{0:T(256)S(1)} copy-done((s32[256]{0:T(256)S(1)}, s32[256]{0:T(256)}, u32[]{:S(2)}) %copy-start.3) | copy-done | bytes 1048
  0.7 0.0 copy-start
  0.7 1.2 %copy-done = bf16[4096,128]{1,0:T(8,128)(2,1)S(1)} copy-done((bf16[4096,128]{1,0:T(8,128)(2,1)S(1)}, bf16[4096,128]{1,0:T(8,128)(2,1)}, u32[]{:S(2)}) %copy-start) | copy-done | bytes 1048600
  1.9 0.0 copy-start.1
  1.9 1.0 %copy-done.1 = bf16[4096,64]{0,1:T(8,128)(2,1)S(1)} copy-done((bf16[4096,64]{0,1:T(8,128)(2,1)S(1)}, bf16[4096,64]{0,1:T(8,128)(2,1)}, u32[]{:S(2)}) %copy-start.1) | copy-done | bytes 524312
  2.9 0.0 copy-start.2
  2.9 0.9 %copy-done.2 = bf16[256,256]{1,0:T(8,128)(2,1)S(1)} copy-done((bf16[256,256]{1,0:T(8,128)(2,1)S(1)}, bf16[256,256]{1,0:T(8,128)(2,1)}, u32[]{:S(2)}) %copy-start.2) | copy-done | bytes 131096
  3.9 24.6 %shard_map.46 = bf16[4096,128]{1,0:T(8,128)(2,1)S(1)} custom-call(bf16[4096,128]{1,0:T(8,128)(2,1)S(1)} %copy-done, bf16[64,4096]{1,0:T(8,128)(2,1)S(1)} %bitcast.2, bf16[256,256]{1,0:T(8,128)(2,1)S(1)} %copy-done.2, s32[1,256]{1,0:T(1,128)S(1)} %bitcast.3), custom_call_target="tpu_custom_call" | custom-call | tf_op jit(solution)/shard_map/pallas_call | solution.py:265
  28.4 1.0 %copy.6 = bf16[4096,128]{1,0:T(8,128)(2,1)} copy(bf16[4096,128]{1,0:T(8,128)(2,1)S(1)} %shard_map.46) | data formatting | bytes 2097152
Async XLA Ops:
  0.0 0.7 %copy-start.3 = (s32[256]{0:T(256)S(1)}, s32[256]{0:T(256)}, u32[]{:S(2)}) copy-start(s32[256]{0:T(256)} %param.7) | copy-start | bytes 3076
  0.7 1.2 %copy-start = (bf16[4096,128]{1,0:T(8,128)(2,1)S(1)}, bf16[4096,128]{1,0:T(8,128)(2,1)}, u32[]{:S(2)}) copy-start(bf16[4096,128]{1,0:T(8,128)(2,1)} %a_hbm.1) | copy-start | bytes 3145732
  1.9 1.0 %copy-start.1 = (bf16[4096,64]{0,1:T(8,128)(2,1)S(1)}, bf16[4096,64]{0,1:T(8,128)(2,1)}, u32[]{:S(2)}) copy-start(bf16[4096,64]{0,1:T(8,128)(2,1)} %param.5) | copy-start | bytes 1572868
  2.9 0.9 %copy-start.2 = (bf16[256,256]{1,0:T(8,128)(2,1)S(1)}, bf16[256,256]{1,0:T(8,128)(2,1)}, u32[]{:S(2)}) copy-start(bf16[256,256]{1,0:T(8,128)(2,1)} %inv_hbm.1) | copy-start | bytes 393220

commit v2 on v1

--- a/solution.py
+++ b/solution.py
@@ -40,9 +40,9 @@
 
 def kernel(
     n_prow, n_pcol, chunks,
-    a_hbm, l_hbm, inv_hbm, pv_ref, out_hbm,
-    a_v, l_full, inv_v, out_v, part, got, mine, tops, origs,
-    load_sem, out_sem, own_sem,
+    a_hbm, l_hbm, inv_hbm, pv_hbm, out_v,
+    a_v, l_full, inv_v, pv_ref, part, got, mine, tops, origs,
+    load_sem,
     p1_send, p1_recv, p2_send, p2_recv, o1_send, o1_recv, o2_send, o2_recv,
     y_send, y_recv, m_send, m_recv, f_send, f_recv,
 ):
@@ -68,30 +68,40 @@
     def frm(d):
         return lax.rem(me + n_prow - d, n_prow)
 
+    first = (n_prow - n_red) // 2
+
+    def is_red(index):
+        return (index >= first) & (index < first + n_red)
+
     def if_red(index, fn):
-        if n_red == n_prow:
-            fn()
-        else:
-            pl.when(index < n_red)(fn)
+        pl.when(is_red(index))(fn)
+
+    def slot_of(index):
+        return lax.rem(index + n_prow - first, n_red)
 
     l_load = pltpu.make_async_copy(l_hbm, l_full.at[col], load_sem.at[0])
     a_load = pltpu.make_async_copy(a_hbm, a_v, load_sem.at[1])
     inv_load = pltpu.make_async_copy(inv_hbm, inv_v, load_sem.at[2])
+    pv_load = pltpu.make_async_copy(pv_hbm, pv_ref, load_sem.at[3])
+    pv_load.start()
     l_load.start()
     a_load.start()
     inv_load.start()
 
     barrier = pltpu.get_barrier_semaphore()
     for d in range(1, n_prow):
-        pl.semaphore_signal(barrier, inc=1, device_id=(to(d), col), device_id_type=MESH)
+        @pl.when(is_red(me) | is_red(to(d)))
+        def _():
+            pl.semaphore_signal(barrier, inc=1, device_id=(to(d), col), device_id_type=MESH)
     for d in range(1, n_y):
         pl.semaphore_signal(barrier, inc=1, device_id=(me, y_peer(d)), device_id_type=MESH)
     pl.semaphore_signal(barrier, inc=1, device_id=(me, mate), device_id_type=MESH)
 
+    pv_load.wait()
     top_source, chain, landing = swap_plan(pv_ref[...].astype(F32))
 
     l_load.wait()
-    pl.semaphore_wait(barrier, n_prow - 1 + n_y - 1 + 1)
+    pl.semaphore_wait(barrier, n_y + jnp.where(is_red(me), n_prow - 1, n_red))
 
     def cols(k):
         return pl.ds(k * step, step)
@@ -110,16 +120,14 @@
     o1_copies = [
         pltpu.make_async_remote_copy(
             a_v.at[pl.ds(d * piece, piece)], origs.at[d], o1_send.at[d], o1_recv,
-            device_id=(d, col), device_id_type=MESH)
-        for d in range(1, n_red)
+            device_id=(first + d, col), device_id_type=MESH)
+        for d in range(n_red)
     ]
-    own_copy = pltpu.make_async_copy(a_v.at[pl.ds(0, piece)], origs.at[0], own_sem)
 
     @pl.when(me == 0)
     def _():
         for copy in o1_copies:
             copy.start()
-        own_copy.start()
 
     m_copy.start()
 
@@ -137,11 +145,22 @@
     for d in range(1, n_prow):
         t = to(d)
         p1_copies[d] = pltpu.make_async_remote_copy(
-            part.at[lax.rem(t, n_red)], got.at[d], p1_send.at[d], p1_recv.at[d],
+            part.at[slot_of(t)], got.at[d], p1_send.at[d], p1_recv.at[d],
             device_id=(t, col), device_id_type=MESH)
         if_red(t, p1_copies[d].start)
 
-    slot = lax.rem(me, n_red)
+    f_copies = {}
+
+    def forward(k):
+        for d in range(1, n_y):
+            y_copies[d, k].wait_recv()
+            src = y_from(d)
+            f_copies[d, k] = pltpu.make_async_remote_copy(
+                l_full.at[src, :, cols(k)], l_full.at[src, :, cols(k)],
+                f_send.at[d, k], f_recv.at[d, k], device_id=(me, mate), device_id_type=MESH)
+            f_copies[d, k].start()
+
+    slot = slot_of(me)
     o2_copies, p2_copies = {}, {}
     for d in range(1, n_prow):
         o2_copies[d] = pltpu.make_async_remote_copy(
@@ -151,19 +170,14 @@
             mine, tops.at[slot], p2_send.at[d], p2_recv.at[d],
             device_id=(to(d), col), device_id_type=MESH)
 
-    @pl.when(me == 0)
-    def _():
-        own_copy.wait()
-
-    @pl.when((me > 0) & (me < n_red))
-    def _():
+    def send_orig():
         o1_copies[0].wait_recv()
-
-    def send_orig():
         for d in range(1, n_prow):
             o2_copies[d].start()
 
     if_red(me, send_orig)
+    forward(0)
+    forward(1)
 
     def reduce_and_send():
         acc = part[slot].astype(F32)
@@ -176,6 +190,7 @@
             p2_copies[d].start()
 
     if_red(me, reduce_and_send)
+    forward(2)
 
     for d in range(1, n_prow):
         if_red(frm(d), o2_copies[d].wait_recv)
@@ -188,24 +203,14 @@
         out_v[rows_k, :] = jnp.where(
             both[:, width:] > 0.5, both[:, :width], a_v[rows_k, :].astype(F32)).astype(BF16)
 
+    early = min(5, chunks)
+    for k in range(3, early):
+        forward(k)
     for d in range(1, n_prow):
         if_red(frm(d), p2_copies[d].wait_recv)
     inv_load.wait()
     u_block = jnp.dot(
         inv_v[...], tops[...].reshape(nb, width), preferred_element_type=F32).astype(BF16)
-
-    f_copies = {}
-
-    def forward(k):
-        for d in range(1, n_y):
-            y_copies[d, k].wait_recv()
-            src = y_from(d)
-            f_copies[d, k] = pltpu.make_async_remote_copy(
-                l_full.at[src, :, cols(k)], l_full.at[src, :, cols(k)],
-                f_send.at[d, k], f_recv.at[d, k], device_id=(me, mate), device_id_type=MESH)
-            f_copies[d, k].start()
-
-    out_copies = []
 
     def finish(k):
         for d in range(1, n_y):
@@ -220,16 +225,16 @@
             @pl.when(me == 0)
             def _():
                 out_v[pl.ds(k * step, top), :] = u_block[k * step:k * step + top, :]
-        copy = pltpu.make_async_copy(out_v.at[rows_k], out_hbm.at[rows_k], out_sem.at[k])
-        copy.start()
-        out_copies.append(copy)
-
-    forward(0)
+
     m_copy.wait_recv()
-    for k in range(1, chunks):
+    done = 0
+    for k in range(early, chunks):
         forward(k)
-        finish(k - 1)
-    finish(chunks - 1)
+        while done < k:
+            finish(done)
+            done += 1
+    for k in range(done, chunks):
+        finish(k)
 
     @pl.when(me == 0)
     def _():
@@ -249,35 +254,37 @@
     for key in y_copies:
         y_copies[key].wait_send()
         f_copies[key].wait_send()
-    for copy in out_copies:
-        copy.wait()
+
+
+def hbm(array):
+    return pltpu.with_memory_space_constraint(array, pltpu.HBM)
 
 
 def body(n_prow, n_pcol, a_matrix, l_panel, l_inverse, pivots):
     rows, width = a_matrix.shape
     nb = l_inverse.shape[0]
     depth = l_panel.shape[1]
-    piece = max(16, nb // n_prow)
-    n_red = nb // piece
+    n_red = min(n_prow // 2, nb // 16)
+    piece = nb // n_red
     n_y = n_pcol // CORES
     chunks = min(8, rows // 128)
     dma = pltpu.SemaphoreType.DMA
     return pl.pallas_call(
         functools.partial(kernel, n_prow, n_pcol, chunks),
         out_shape=jax.ShapeDtypeStruct((rows, width), BF16),
-        in_specs=[pl.BlockSpec(memory_space=pl.ANY)] * 3 + [pl.BlockSpec(memory_space=pltpu.VMEM)],
-        out_specs=pl.BlockSpec(memory_space=pl.ANY),
+        in_specs=[pl.BlockSpec(memory_space=pl.ANY)] * 4,
+        out_specs=pl.BlockSpec(memory_space=pltpu.VMEM),
         scratch_shapes=[
             pltpu.VMEM((rows, width), BF16),
             pltpu.VMEM((n_pcol, depth, rows), BF16),
             pltpu.VMEM((nb, nb), BF16),
-            pltpu.VMEM((rows, width), BF16),
+            pltpu.VMEM((1, nb), jnp.int32),
             pltpu.VMEM((n_red, piece, width), BF16),
             pltpu.VMEM((n_prow, piece, width), BF16),
             pltpu.VMEM((piece, width), BF16),
             pltpu.VMEM((n_red, piece, width), BF16),
             pltpu.VMEM((n_red, piece, width), BF16),
-            dma((3,)), dma((chunks,)), dma,
+            dma((4,)),
             dma((n_prow,)), dma((n_prow,)), dma((n_prow,)), dma((n_prow,)),
             dma((n_red,)), dma, dma((n_prow,)), dma((n_prow,)),
             dma((n_y, chunks)), dma((n_y, chunks)), dma, dma,
@@ -285,7 +292,7 @@
         ],
         compiler_params=pltpu.CompilerParams(
             collective_id=0, has_side_effects=True, vmem_limit_bytes=24 * 2 ** 20),
-    )(a_matrix, l_panel.T, l_inverse, pivots.reshape(1, nb))
+    )(hbm(a_matrix), hbm(l_panel.T), hbm(l_inverse), hbm(pivots.reshape(1, nb)))
 
 
 def solution(mesh):

time: 29.6 us -> 21.7 us (0.73)
  Pallas kernels: 24.6 us -> 20.3 us
  local copies, waits for them, and re-layouts: 4.82 us -> 0.97 us
    pallas_call x1, Pallas kernels: 24.6 us -> 20.3 us  [body(): pl.pallas_call(functools.partial(kernel, n_prow, n_pcol, chunks), out_sha...]
    unnamed x9 -> x1, local copies, waits for them, and re-layouts: 4.82 us -> 0.97 us
where the time goes in v2:
time: 21.7 us; the launch traced here: 21.3 us
  Pallas kernels  20.3 us (94%)
  local copies, waits for them, and re-layouts  0.97 us (4%)
    pallas_call x1, Pallas kernels, body(): pl.pallas_call(functools.partial(kernel, n_prow, n_pcol, chunks), out_sha...  20.3 us
    unnamed x1, local copies, waits for them, and re-layouts  0.97 us

profile of v2, /device:TPU:0, one launch (start us, length us, event | category | flops | bytes accessed | tf_op | source)
XLA Modules:
  0.0 21.3 jit_solution(13457757551443347391)
XLA Ops:
  0.0 20.3 %shard_map.46 = bf16[4096,128]{1,0:T(8,128)(2,1)S(1)} custom-call(bf16[4096,128]{1,0:T(8,128)(2,1)} %a_hbm.1, bf16[64,4096]{1,0:T(8,128)(2,1)} %bitcast.2, bf16[256,256]{1,0:T(8,128)(2,1)} %inv_hbm.1, s32[1,256]{1,0:T(1,128)} %bitcast.3), custom_call_target="tpu_custom_call" | custom-call | tf_op jit(solution)/shard_map/pallas_call | solution.py:272
  20.3 1.0 %copy.6 = bf16[4096,128]{1,0:T(8,128)(2,1)} copy(bf16[4096,128]{1,0:T(8,128)(2,1)S(1)} %shard_map.46) | data formatting | bytes 2097152
